TPU v7x, 32 devices: a whole 2x2x4 slice. The times are simulated.
32 devices in a mesh: section: 8 (over z, core), expert: 4 (over y, x).
Axes of the slice: x: 2, y: 2, z: 4, core: 2. Of those that a mesh axis runs over, the one named last changes fastest.
Arguments:
- state: bfloat16 [8, 512, 2048], P('section', 'expert'), may hold values from -6 to 6
- norm_gain: float32 [8, 2048], P('section'), may hold values from 0.25 to 1.75
- expert_in: bfloat16 [8, 4, 2048, 1536], P('section', 'expert'), may hold values from -0.125 to 0.125
- expert_out: bfloat16 [8, 4, 768, 2048], P('section', 'expert'), may hold values from -0.21875 to 0.21875
- route_ids: int32 [3, 8, 512, 6], P(None, 'section', 'expert'), may hold values from 0 to 63, all different within a row
- route_weights: float32 [3, 8, 512, 6], P(None, 'section', 'expert'), may hold values from 0.3 to 3
Outputs:
- state_out: bfloat16 [8, 512, 2048], P('section', 'expert')
Inputs may be any that keep to these rules, and one draw needn't show every extreme that they name: `route_ids`: each token names 6 different experts.
All inputs are finite; a program needn't handle non-finite values.
Results may differ from a plain program's by a relative error of at most 0.02.
Values may be sent and summed in bfloat16 or wider, within the bound.
A program may use at most 64 MiB of HBM per device.

v0:
```python
import functools

import jax
import jax.numpy as jnp
from jax import lax
from jax.experimental import pallas as pl
from jax.experimental.pallas import tpu as pltpu
from jax.sharding import PartitionSpec as P

epsilon = 1e-06
COLUMN_SHARES = (1, 1, 1, 1)
SLOT_SHARES = (1, 1)
MESH = pl.DeviceIdType.MESH


def cuts(total, shares):
    whole = sum(shares)
    ends = [total * sum(shares[: i + 1]) // whole for i in range(len(shares))]
    starts = [0] + ends[:-1]
    return [(a, b - a) for a, b in zip(starts, ends)]


def relay_kernel(
    sections,
    experts,
    state_hbm,
    gain_hbm,
    win_hbm,
    wout_hbm,
    ids_hbm,
    wts_hbm,
    out_ref,
    win,
    wout,
    gain,
    ids,
    wts,
    ids_before,
    wts_before,
    state,
    hcur,
    arrive,
    first,
    pick,
    comb,
    sendbuf,
    recvbuf,
    retsend,
    acc,
    load_sem,
    win_sem,
    state_sem,
    route_ss,
    route_rs,
    disp_ss,
    disp_rs,
    ret_ss,
    ret_rs,
    h_ss,
    h_rs,
):
    ticks, top = ids.shape[:2]
    tokens = state[0].shape[0]
    columns = cuts(state_hbm.shape[2], COLUMN_SHARES)
    width = state_hbm.shape[2]
    chunks = len(columns)
    hidden_units = wout.shape[0]
    capacity = tokens // 4
    slots = experts * capacity
    parts = cuts(capacity, SLOT_SHARES)

    section = lax.axis_index("section")
    me = lax.axis_index("expert")
    after = lax.rem(section + 1, sections)
    before = lax.rem(section + sections - 1, sections)
    others = range(1, experts)

    barrier = pltpu.get_barrier_semaphore()
    for d in others:
        pl.semaphore_signal(
            barrier,
            inc=1,
            device_id={"section": section, "expert": lax.rem(me + d, experts)},
            device_id_type=MESH,
        )
    for e in range(experts):
        pl.semaphore_signal(
            barrier, inc=1, device_id={"section": before, "expert": e}, device_id_type=MESH
        )

    load_ids = pltpu.make_async_copy(ids_hbm, ids, load_sem.at[0])
    load_wts = pltpu.make_async_copy(wts_hbm, wts, load_sem.at[1])
    load_gain = pltpu.make_async_copy(gain_hbm, gain, load_sem.at[2])
    load_out = pltpu.make_async_copy(wout_hbm.at[0, 0], wout, load_sem.at[3])

    def load_state(c):
        start, size = columns[c]
        return pltpu.make_async_copy(
            state_hbm.at[0, :, pl.ds(start, size)], state[c], state_sem.at[c]
        )

    def load_in(c):
        rows = pl.ds(*columns[c])
        return pltpu.make_async_copy(win_hbm.at[0, 0, rows], win.at[rows], win_sem.at[c])

    load_ids.start()
    for c in range(chunks):
        load_state(c).start()
    load_wts.start()
    load_gain.start()
    for c in range(chunks):
        load_in(c).start()
    load_out.start()

    slot_row = lax.broadcasted_iota(jnp.int32, (slots, tokens), 0)
    expert_of = jnp.zeros((slots, tokens), jnp.int32)
    slot_of = slot_row
    for low, half in parts:
        for e in range(experts):
            start = low * experts + e * half
            inside = slot_row >= start
            expert_of = jnp.where(inside, e, expert_of)
            slot_of = jnp.where(inside, slot_row - start + low, slot_of)
    slot_of = slot_of.astype(jnp.float32)
    row_i = lax.broadcasted_iota(jnp.int32, (tokens, tokens), 0)
    col_i = lax.broadcasted_iota(jnp.int32, (tokens, tokens), 1)
    earlier = jnp.where(row_i < col_i, 1.0, 0.0).astype(jnp.bfloat16)

    def kept_slots(ids_ref, t):
        hit = jnp.zeros((slots, tokens), jnp.float32)
        for k in range(top):
            hit = jnp.where(ids_ref[t, k] == expert_of, 1.0, hit)
        rank = jnp.dot(hit.astype(jnp.bfloat16), earlier, preferred_element_type=jnp.float32)
        return jnp.where(rank == slot_of, hit, 0.0)

    def make_comb(t):
        mix = jnp.zeros((slots, tokens), jnp.float32)
        for k in range(top):
            mix = jnp.where(ids_before[t, k] == expert_of, wts_before[t, k], mix)
        weighted = kept_slots(ids_before, t) * mix
        comb[t] = jnp.transpose(weighted).astype(jnp.bfloat16)

    def make_pick(t):
        keep = kept_slots(ids, t).astype(jnp.bfloat16)
        mixed = jnp.dot(keep, comb[t - 1], preferred_element_type=jnp.float32)
        pick[t - 1, :, pl.ds(0, slots)] = mixed.astype(jnp.bfloat16)
        pick[t - 1, :, pl.ds(slots, tokens)] = keep

    def route_copies():
        return [
            pltpu.make_async_remote_copy(
                src_ref=mine,
                dst_ref=theirs,
                send_sem=route_ss.at[i],
                recv_sem=route_rs.at[i],
                device_id={"section": after, "expert": me},
                device_id_type=MESH,
            )
            for i, (mine, theirs) in enumerate(((ids, ids_before), (wts, wts_before)))
        ]

    def h_copy(t, c):
        return pltpu.make_async_remote_copy(
            src_ref=state[c] if t == 0 else hcur[c].at[t - 1],
            dst_ref=arrive[c].at[t, pl.ds(slots, tokens)],
            send_sem=h_ss.at[t, c],
            recv_sem=h_rs.at[t, c],
            device_id={"section": after, "expert": me},
            device_id_type=MESH,
        )

    def part_rows(p, e):
        low, half = parts[p]
        return pl.ds(pl.multiple_of(low * experts + e * half, 8), half)

    def part_all(p):
        low, half = parts[p]
        return pl.ds(low * experts, half * experts)

    def send_rows(t, p, c):
        for d in others:
            peer = lax.rem(me + d, experts)
            pltpu.make_async_remote_copy(
                src_ref=sendbuf[c].at[t, part_rows(p, peer)],
                dst_ref=recvbuf[c].at[t, part_rows(p, me)],
                send_sem=disp_ss.at[t, c],
                recv_sem=disp_rs.at[t, p, c],
                device_id={"section": section, "expert": peer},
                device_id_type=MESH,
            ).start()

    def await_rows(t, p, c):
        low, half = parts[p]
        block = recvbuf[c].at[t, pl.ds(low * experts, (experts - 1) * half)]
        pltpu.make_async_remote_copy(
            src_ref=block,
            dst_ref=block,
            send_sem=disp_ss.at[t, c],
            recv_sem=disp_rs.at[t, p, c],
            device_id={"section": section, "expert": lax.rem(me + 1, experts)},
            device_id_type=MESH,
        ).wait_recv()

    def send_served(t, p, c):
        for d in (*others, 0):
            peer = lax.rem(me + d, experts)
            pltpu.make_async_remote_copy(
                src_ref=retsend[c].at[t, part_rows(p, peer)],
                dst_ref=arrive[c].at[t, part_rows(p, me)],
                send_sem=ret_ss.at[t, c],
                recv_sem=ret_rs.at[t, c],
                device_id={"section": after, "expert": peer},
                device_id_type=MESH,
            ).start()

    def served_copy(t, c):
        return pltpu.make_async_remote_copy(
            src_ref=retsend[c].at[t],
            dst_ref=arrive[c].at[t, pl.ds(0, slots)],
            send_sem=ret_ss.at[t, c],
            recv_sem=ret_rs.at[t, c],
            device_id={"section": before, "expert": me},
            device_id_type=MESH,
        )

    def fill(t, c, picker, source):
        rows = jnp.dot(picker, source, preferred_element_type=jnp.float32)
        sendbuf[c][t] = rows.astype(jnp.bfloat16)

    def keep_own(t, c):
        for p in range(len(parts)):
            own = part_rows(p, me)
            recvbuf[c][t, own, :] = sendbuf[c][t, own, :]

    def dispatch(t, c):
        send_rows(t, 0, c)
        if c == chunks - 1:
            for p in range(1, len(parts)):
                for late in range(chunks):
                    send_rows(t, p, late)

    load_ids.wait()
    first[...] = kept_slots(ids, 0).astype(jnp.bfloat16)
    for c in range(chunks):
        load_state(c).wait()
        fill(0, c, first[...], state[c][...])
        keep_own(0, c)
    load_wts.wait()
    pl.semaphore_wait(barrier, experts - 1 + experts)
    for c in range(chunks):
        dispatch(0, c)
    for copy in route_copies():
        copy.start()
    for c in range(chunks):
        h_copy(0, c).start()
    for copy in route_copies():
        copy.wait_recv()
    for t in range(ticks):
        make_comb(t)
    for t in range(1, ticks):
        make_pick(t)

    load_gain.wait()
    for t in range(ticks):
        for p in range(len(parts)):
            rows = part_all(p)
            group = rows.size
            squares = jnp.zeros((group, 1), jnp.float32)
            for c in range(chunks):
                cols = pl.ds(*columns[c])
                if t == 0 and p == 0:
                    load_in(c).wait()
                await_rows(t, p, c)
                wide = recvbuf[c][t, rows, :].astype(jnp.float32)
                squares = squares + jnp.sum(wide * wide, axis=-1, keepdims=True)
                scaled = (wide * gain[:, cols]).astype(jnp.bfloat16)
                part = jnp.dot(scaled, win[cols, :], preferred_element_type=jnp.float32)
                if c == 0:
                    acc[pl.ds(0, group), :] = part
                else:
                    acc[pl.ds(0, group), :] += part
            rescale = lax.rsqrt(squares / width + epsilon)
            gate = acc[pl.ds(0, group), :hidden_units] * rescale
            up = acc[pl.ds(0, group), hidden_units:] * rescale
            activated = (gate / (1.0 + jnp.exp(-gate)) * up).astype(jnp.bfloat16)
            if t == 0 and p == 0:
                load_out.wait()
            for c in range(chunks):
                served = jnp.dot(
                    activated, wout[:, pl.ds(*columns[c])], preferred_element_type=jnp.float32
                )
                retsend[c][t, rows, :] = served.astype(jnp.bfloat16)
                send_served(t, p, c)
        for c in range(chunks):
            h_copy(t, c).wait_recv()
            served_copy(t, c).wait_recv()
            if t < ticks - 1:
                fill(t + 1, c, pick[t], arrive[c][t])
                dispatch(t + 1, c)
            branch = jnp.dot(
                comb[t], arrive[c][t, pl.ds(0, slots)], preferred_element_type=jnp.float32
            )
            stay = arrive[c][t, pl.ds(slots, tokens)].astype(jnp.float32)
            fresh = (stay + branch).astype(jnp.bfloat16)
            if t == ticks - 1:
                out_ref[0, :, pl.ds(*columns[c])] = fresh
            else:
                hcur[c][t] = fresh
                h_copy(t + 1, c).start()
                keep_own(t + 1, c)

    for copy in route_copies():
        copy.wait_send()
    for t in range(ticks):
        for c in range(chunks):
            h_copy(t, c).wait_send()
            sent = sendbuf[c].at[t, pl.ds(0, slots - capacity)]
            pltpu.make_async_remote_copy(
                src_ref=sent,
                dst_ref=sent,
                send_sem=disp_ss.at[t, c],
                recv_sem=disp_rs.at[t, 0, c],
                device_id={"section": after, "expert": me},
                device_id_type=MESH,
            ).wait_send()
            served_copy(t, c).wait_send()


def on_device(sections, experts, state, norm_gain, expert_in, expert_out, route_ids, route_weights):
    ticks, _, _, top = route_ids.shape
    tokens, width = state.shape[1:]
    inner = expert_in.shape[3]
    hidden_units = expert_out.shape[2]
    slots = experts * (tokens // 4)
    columns = cuts(width, COLUMN_SHARES)
    chunks, parts = len(columns), len(SLOT_SHARES)
    widest = max(size for _, size in cuts(tokens // 4, SLOT_SHARES)) * experts
    bf16 = jnp.bfloat16
    hbm = pl.BlockSpec(memory_space=pltpu.HBM)
    dma = pltpu.SemaphoreType.DMA

    def per_chunk(*shape):
        return [pltpu.VMEM((*shape, size), bf16) for _, size in columns]

    def in_hbm(x):
        return pltpu.with_memory_space_constraint(x, pltpu.HBM)

    return pl.pallas_call(
        functools.partial(relay_kernel, sections, experts),
        out_shape=pltpu.VMEM(state.shape, state.dtype),
        in_specs=[hbm] * 6,
        out_specs=pl.BlockSpec(memory_space=pltpu.VMEM),
        scratch_shapes=[
            pltpu.VMEM((width, inner), bf16),
            pltpu.VMEM((hidden_units, width), bf16),
            pltpu.VMEM((1, width), jnp.float32),
            pltpu.VMEM((ticks, top, 1, tokens), jnp.int32),
            pltpu.VMEM((ticks, top, 1, tokens), jnp.float32),
            pltpu.VMEM((ticks, top, 1, tokens), jnp.int32),
            pltpu.VMEM((ticks, top, 1, tokens), jnp.float32),
            per_chunk(tokens),
            per_chunk(max(ticks - 1, 1), tokens),
            per_chunk(ticks, slots + tokens),
            pltpu.VMEM((slots, tokens), bf16),
            pltpu.VMEM((max(ticks - 1, 1), slots, slots + tokens), bf16),
            pltpu.VMEM((ticks, tokens, slots), bf16),
            per_chunk(ticks, slots),
            per_chunk(ticks, slots),
            per_chunk(ticks, slots),
            pltpu.VMEM((widest, inner), jnp.float32),
            dma((4,)),
            dma((chunks,)),
            dma((chunks,)),
            dma((2,)),
            dma((2,)),
            dma((ticks, chunks)),
            dma((ticks, parts, chunks)),
            dma((ticks, chunks)),
            dma((ticks, chunks)),
            dma((ticks, chunks)),
            dma((ticks, chunks)),
        ],
        compiler_params=pltpu.CompilerParams(
            collective_id=0, has_side_effects=True, vmem_limit_bytes=48 * 2**20
        ),
        name="relay",
    )(
        in_hbm(state),
        in_hbm(norm_gain),
        in_hbm(expert_in),
        in_hbm(expert_out),
        in_hbm(jnp.transpose(route_ids, (0, 3, 1, 2))),
        in_hbm(jnp.transpose(route_weights, (0, 3, 1, 2))),
    )


def solution(mesh):
    in_specs = (
        P("section", "expert", None),
        P("section", None),
        P("section", "expert", None, None),
        P("section", "expert", None, None),
        P(None, "section", "expert", None),
        P(None, "section", "expert", None),
    )
    out_specs = P("section", "expert", None)
    return jax.shard_map(
        functools.partial(on_device, mesh.shape["section"], mesh.shape["expert"]),
        mesh=mesh,
        in_specs=in_specs,
        out_specs=out_specs,
        check_vma=False,
    )
```

profile of v0, /device:TPU:0, one launch (start us, length us, event | category | flops | bytes accessed | tf_op | source)
XLA Modules:
  0.0 47.4 jit_solution(8007485369083195353)
XLA Ops:
  0.0 46.6 %relay.1 = bf16[1,128,2048]{2,1,0:T(8,128)(2,1)S(1)} custom-call(bf16[1,128,2048]{2,1,0:T(8,128)(2,1)} %state_hbm.1, f32[1,2048]{1,0:T(1,128)} %gain_hbm.1, bf16[1,1,2048,1536]{3,2,1,0:T(8,128)(2,1)} %win_hbm.1, bf16[1,1,768,2048]{3,2,1,0:T(8,128)(2,1)} %wout_hbm.1, s32[3,6,1,128]{3,2,1,0:T(1,128)} %bitcast.2, f32[3,6,1,128]{3,2,1,0:T(1,128)} %bitcast.3), custom_call_target="tpu_custom_call" | custom-call | tf_op jit(solution)/shard_map/relay/pallas_call | solution.py:348
  46.6 0.8 %copy.8 = bf16[1,128,2048]{2,1,0:T(8,128)(2,1)} copy(bf16[1,128,2048]{2,1,0:T(8,128)(2,1)S(1)} %relay.1) | data formatting | bytes 1048576
where the time goes:
time: 48 us; the launch traced here: 47.4 us
  Pallas kernels  46.6 us (97%)
  local copies, waits for them, and re-layouts  0.8 us (2%)
    pallas_call x1, Pallas kernels, on_device(): pl.pallas_call(functools.partial(relay_kernel, sections, experts), out_sh...  46.6 us

commit v1 on v0

--- a/solution.py
+++ b/solution.py
@@ -10,6 +10,8 @@
 epsilon = 1e-06
 COLUMN_SHARES = (1, 1, 1, 1)
 SLOT_SHARES = (1, 1)
+DISPATCH_RUNS = ((1, 1, 1, 1), (1, 1, 1, 1))
+RETURN_RUNS = ((2, 2), (1, 1, 1, 1))
 MESH = pl.DeviceIdType.MESH
 
 
@@ -18,6 +20,11 @@
     ends = [total * sum(shares[: i + 1]) // whole for i in range(len(shares))]
     starts = [0] + ends[:-1]
     return [(a, b - a) for a, b in zip(starts, ends)]
+
+
+def runs(lengths):
+    ends = [sum(lengths[: i + 1]) for i in range(len(lengths))]
+    return [(b - n, b) for b, n in zip(ends, lengths)]
 
 
 def relay_kernel(
@@ -57,10 +64,9 @@
     ret_ss,
     ret_rs,
     h_ss,
-    h_rs,
 ):
     ticks, top = ids.shape[:2]
-    tokens = state[0].shape[0]
+    tokens = state.shape[0]
     columns = cuts(state_hbm.shape[2], COLUMN_SHARES)
     width = state_hbm.shape[2]
     chunks = len(columns)
@@ -68,19 +74,44 @@
     capacity = tokens // 4
     slots = experts * capacity
     parts = cuts(capacity, SLOT_SHARES)
+    disp_runs = [runs(lengths) for lengths in DISPATCH_RUNS]
+    ret_runs = [runs(lengths) for lengths in RETURN_RUNS]
+
+    def disp_sem(p, low):
+        return sum(map(len, disp_runs[:p])) + [a for a, _ in disp_runs[p]].index(low)
+
+    def ret_sem(p, low):
+        return sum(map(len, ret_runs[:p])) + [a for a, _ in ret_runs[p]].index(low)
+
+    def span(low, high):
+        start = columns[low][0]
+        return pl.ds(start, sum(columns[high - 1]) - start)
 
     section = lax.axis_index("section")
     me = lax.axis_index("expert")
     after = lax.rem(section + 1, sections)
     before = lax.rem(section + sections - 1, sections)
-    others = range(1, experts)
+    lanes = max(k for k in range(1, experts + 1) if experts % k == 0 and k * k <= experts)
+    files = experts // lanes
+    steps = [(i, j) for i in range(lanes) for j in range(files)]
+
+    def hops(step):
+        i, j = step
+        return min(i, lanes - i) + min(j, files - j)
+
+    def peer_at(step):
+        i, j = step
+        return lax.rem(me // files + i, lanes) * files + lax.rem(lax.rem(me, files) + j, files)
+
+    steps_d = sorted([s for s in steps if s != (0, 0)], key=lambda s: (hops(s), s), reverse=True)
+    steps_r = sorted(steps, key=lambda s: (hops(s), s), reverse=True)
 
     barrier = pltpu.get_barrier_semaphore()
-    for d in others:
+    for step in steps_d:
         pl.semaphore_signal(
             barrier,
             inc=1,
-            device_id={"section": section, "expert": lax.rem(me + d, experts)},
+            device_id={"section": section, "expert": peer_at(step)},
             device_id_type=MESH,
         )
     for e in range(experts):
@@ -94,9 +125,9 @@
     load_out = pltpu.make_async_copy(wout_hbm.at[0, 0], wout, load_sem.at[3])
 
     def load_state(c):
-        start, size = columns[c]
+        cols = pl.ds(*columns[c])
         return pltpu.make_async_copy(
-            state_hbm.at[0, :, pl.ds(start, size)], state[c], state_sem.at[c]
+            state_hbm.at[0, :, cols], state.at[:, cols], state_sem.at[c]
         )
 
     def load_in(c):
@@ -108,9 +139,6 @@
         load_state(c).start()
     load_wts.start()
     load_gain.start()
-    for c in range(chunks):
-        load_in(c).start()
-    load_out.start()
 
     slot_row = lax.broadcasted_iota(jnp.int32, (slots, tokens), 0)
     expert_of = jnp.zeros((slots, tokens), jnp.int32)
@@ -160,11 +188,12 @@
         ]
 
     def h_copy(t, c):
+        cols = pl.ds(*columns[c])
         return pltpu.make_async_remote_copy(
-            src_ref=state[c] if t == 0 else hcur[c].at[t - 1],
-            dst_ref=arrive[c].at[t, pl.ds(slots, tokens)],
-            send_sem=h_ss.at[t, c],
-            recv_sem=h_rs.at[t, c],
+            src_ref=state.at[:, cols] if t == 0 else hcur.at[t - 1, :, cols],
+            dst_ref=arrive.at[t, pl.ds(slots, tokens), cols],
+            send_sem=h_ss,
+            recv_sem=ret_rs.at[t, ret_sem(len(parts) - 1, c)],
             device_id={"section": after, "expert": me},
             device_id_type=MESH,
         )
@@ -177,80 +206,100 @@
         low, half = parts[p]
         return pl.ds(low * experts, half * experts)
 
-    def send_rows(t, p, c):
-        for d in others:
-            peer = lax.rem(me + d, experts)
+    def send_rows(t, p, low, high):
+        for step in steps_d:
+            peer = peer_at(step)
             pltpu.make_async_remote_copy(
-                src_ref=sendbuf[c].at[t, part_rows(p, peer)],
-                dst_ref=recvbuf[c].at[t, part_rows(p, me)],
-                send_sem=disp_ss.at[t, c],
-                recv_sem=disp_rs.at[t, p, c],
+                src_ref=sendbuf.at[t, part_rows(p, peer), span(low, high)],
+                dst_ref=recvbuf.at[t, part_rows(p, me), span(low, high)],
+                send_sem=disp_ss,
+                recv_sem=disp_rs.at[t, disp_sem(p, low)],
                 device_id={"section": section, "expert": peer},
                 device_id_type=MESH,
             ).start()
 
     def await_rows(t, p, c):
-        low, half = parts[p]
-        block = recvbuf[c].at[t, pl.ds(low * experts, (experts - 1) * half)]
-        pltpu.make_async_remote_copy(
-            src_ref=block,
-            dst_ref=block,
-            send_sem=disp_ss.at[t, c],
-            recv_sem=disp_rs.at[t, p, c],
-            device_id={"section": section, "expert": lax.rem(me + 1, experts)},
-            device_id_type=MESH,
-        ).wait_recv()
+        first_row, half = parts[p]
+        for low, high in disp_runs[p]:
+            if low == c:
+                block = recvbuf.at[
+                    t, pl.ds(first_row * experts, (experts - 1) * half), span(low, high)
+                ]
+                pltpu.make_async_remote_copy(
+                    src_ref=block,
+                    dst_ref=block,
+                    send_sem=disp_ss,
+                    recv_sem=disp_rs.at[t, disp_sem(p, low)],
+                    device_id={"section": section, "expert": lax.rem(me + 1, experts)},
+                    device_id_type=MESH,
+                ).wait_recv()
 
     def send_served(t, p, c):
-        for d in (*others, 0):
-            peer = lax.rem(me + d, experts)
-            pltpu.make_async_remote_copy(
-                src_ref=retsend[c].at[t, part_rows(p, peer)],
-                dst_ref=arrive[c].at[t, part_rows(p, me)],
-                send_sem=ret_ss.at[t, c],
-                recv_sem=ret_rs.at[t, c],
-                device_id={"section": after, "expert": peer},
-                device_id_type=MESH,
-            ).start()
-
-    def served_copy(t, c):
-        return pltpu.make_async_remote_copy(
-            src_ref=retsend[c].at[t],
-            dst_ref=arrive[c].at[t, pl.ds(0, slots)],
-            send_sem=ret_ss.at[t, c],
-            recv_sem=ret_rs.at[t, c],
-            device_id={"section": before, "expert": me},
-            device_id_type=MESH,
-        )
+        for low, high in ret_runs[p]:
+            if high == c + 1:
+                for step in steps_r:
+                    peer = peer_at(step)
+                    pltpu.make_async_remote_copy(
+                        src_ref=retsend.at[t, part_rows(p, peer), span(low, high)],
+                        dst_ref=arrive.at[t, part_rows(p, me), span(low, high)],
+                        send_sem=ret_ss,
+                        recv_sem=ret_rs.at[t, ret_sem(p, low)],
+                        device_id={"section": after, "expert": peer},
+                        device_id_type=MESH,
+                    ).start()
+
+    def await_served(t, c):
+        last = len(parts) - 1
+        for p in range(len(parts)):
+            for low, high in ret_runs[p]:
+                if low == c:
+                    rows = part_all(p)
+                    if p == last:
+                        rows = pl.ds(rows.start, rows.size + tokens)
+                    block = arrive.at[t, rows, span(low, high)]
+                    pltpu.make_async_remote_copy(
+                        src_ref=block,
+                        dst_ref=block,
+                        send_sem=ret_ss,
+                        recv_sem=ret_rs.at[t, ret_sem(p, low)],
+                        device_id={"section": before, "expert": me},
+                        device_id_type=MESH,
+                    ).wait_recv()
 
     def fill(t, c, picker, source):
         rows = jnp.dot(picker, source, preferred_element_type=jnp.float32)
-        sendbuf[c][t] = rows.astype(jnp.bfloat16)
+        sendbuf[t, :, pl.ds(*columns[c])] = rows.astype(jnp.bfloat16)
 
     def keep_own(t, c):
+        cols = pl.ds(*columns[c])
         for p in range(len(parts)):
             own = part_rows(p, me)
-            recvbuf[c][t, own, :] = sendbuf[c][t, own, :]
+            recvbuf[t, own, cols] = sendbuf[t, own, cols]
 
     def dispatch(t, c):
-        send_rows(t, 0, c)
+        for low, high in disp_runs[0]:
+            if high == c + 1:
+                send_rows(t, 0, low, high)
         if c == chunks - 1:
             for p in range(1, len(parts)):
-                for late in range(chunks):
-                    send_rows(t, p, late)
+                for low, high in disp_runs[p]:
+                    send_rows(t, p, low, high)
 
     load_ids.wait()
     first[...] = kept_slots(ids, 0).astype(jnp.bfloat16)
     for c in range(chunks):
         load_state(c).wait()
-        fill(0, c, first[...], state[c][...])
+        fill(0, c, first[...], state[:, pl.ds(*columns[c])])
         keep_own(0, c)
+    for c in range(chunks):
+        load_in(c).start()
+    load_out.start()
     load_wts.wait()
     pl.semaphore_wait(barrier, experts - 1 + experts)
+    for copy in route_copies():
+        copy.start()
     for c in range(chunks):
         dispatch(0, c)
-    for copy in route_copies():
-        copy.start()
     for c in range(chunks):
         h_copy(0, c).start()
     for copy in route_copies():
@@ -271,7 +320,7 @@
                 if t == 0 and p == 0:
                     load_in(c).wait()
                 await_rows(t, p, c)
-                wide = recvbuf[c][t, rows, :].astype(jnp.float32)
+                wide = recvbuf[t, rows, cols].astype(jnp.float32)
                 squares = squares + jnp.sum(wide * wide, axis=-1, keepdims=True)
                 scaled = (wide * gain[:, cols]).astype(jnp.bfloat16)
                 part = jnp.dot(scaled, win[cols, :], preferred_element_type=jnp.float32)
@@ -289,41 +338,41 @@
                 served = jnp.dot(
                     activated, wout[:, pl.ds(*columns[c])], preferred_element_type=jnp.float32
                 )
-                retsend[c][t, rows, :] = served.astype(jnp.bfloat16)
+                retsend[t, rows, pl.ds(*columns[c])] = served.astype(jnp.bfloat16)
                 send_served(t, p, c)
         for c in range(chunks):
-            h_copy(t, c).wait_recv()
-            served_copy(t, c).wait_recv()
+            cols = pl.ds(*columns[c])
+            await_served(t, c)
             if t < ticks - 1:
-                fill(t + 1, c, pick[t], arrive[c][t])
+                fill(t + 1, c, pick[t], arrive[t, :, cols])
                 dispatch(t + 1, c)
             branch = jnp.dot(
-                comb[t], arrive[c][t, pl.ds(0, slots)], preferred_element_type=jnp.float32
+                comb[t], arrive[t, pl.ds(0, slots), cols], preferred_element_type=jnp.float32
             )
-            stay = arrive[c][t, pl.ds(slots, tokens)].astype(jnp.float32)
+            stay = arrive[t, pl.ds(slots, tokens), cols].astype(jnp.float32)
             fresh = (stay + branch).astype(jnp.bfloat16)
             if t == ticks - 1:
-                out_ref[0, :, pl.ds(*columns[c])] = fresh
+                out_ref[0, :, cols] = fresh
             else:
-                hcur[c][t] = fresh
+                hcur[t, :, cols] = fresh
                 h_copy(t + 1, c).start()
                 keep_own(t + 1, c)
 
     for copy in route_copies():
         copy.wait_send()
-    for t in range(ticks):
-        for c in range(chunks):
-            h_copy(t, c).wait_send()
-            sent = sendbuf[c].at[t, pl.ds(0, slots - capacity)]
-            pltpu.make_async_remote_copy(
-                src_ref=sent,
-                dst_ref=sent,
-                send_sem=disp_ss.at[t, c],
-                recv_sem=disp_rs.at[t, 0, c],
-                device_id={"section": after, "expert": me},
-                device_id_type=MESH,
-            ).wait_send()
-            served_copy(t, c).wait_send()
+    for sent, sem in (
+        (sendbuf.at[:, pl.ds(0, slots - capacity)], disp_ss),
+        (retsend, ret_ss),
+        (arrive.at[:, pl.ds(slots, tokens)], h_ss),
+    ):
+        pltpu.make_async_remote_copy(
+            src_ref=sent,
+            dst_ref=sent,
+            send_sem=sem,
+            recv_sem=disp_rs.at[0, 0],
+            device_id={"section": after, "expert": me},
+            device_id_type=MESH,
+        ).wait_send()
 
 
 def on_device(sections, experts, state, norm_gain, expert_in, expert_out, route_ids, route_weights):
@@ -333,14 +382,11 @@
     hidden_units = expert_out.shape[2]
     slots = experts * (tokens // 4)
     columns = cuts(width, COLUMN_SHARES)
-    chunks, parts = len(columns), len(SLOT_SHARES)
+    chunks = len(columns)
     widest = max(size for _, size in cuts(tokens // 4, SLOT_SHARES)) * experts
     bf16 = jnp.bfloat16
     hbm = pl.BlockSpec(memory_space=pltpu.HBM)
     dma = pltpu.SemaphoreType.DMA
-
-    def per_chunk(*shape):
-        return [pltpu.VMEM((*shape, size), bf16) for _, size in columns]
 
     def in_hbm(x):
         return pltpu.with_memory_space_constraint(x, pltpu.HBM)
@@ -358,27 +404,26 @@
             pltpu.VMEM((ticks, top, 1, tokens), jnp.float32),
             pltpu.VMEM((ticks, top, 1, tokens), jnp.int32),
             pltpu.VMEM((ticks, top, 1, tokens), jnp.float32),
-            per_chunk(tokens),
-            per_chunk(max(ticks - 1, 1), tokens),
-            per_chunk(ticks, slots + tokens),
+            pltpu.VMEM((tokens, width), bf16),
+            pltpu.VMEM((max(ticks - 1, 1), tokens, width), bf16),
+            pltpu.VMEM((ticks, slots + tokens, width), bf16),
             pltpu.VMEM((slots, tokens), bf16),
             pltpu.VMEM((max(ticks - 1, 1), slots, slots + tokens), bf16),
             pltpu.VMEM((ticks, tokens, slots), bf16),
-            per_chunk(ticks, slots),
-            per_chunk(ticks, slots),
-            per_chunk(ticks, slots),
+            pltpu.VMEM((ticks, slots, width), bf16),
+            pltpu.VMEM((ticks, slots, width), bf16),
+            pltpu.VMEM((ticks, slots, width), bf16),
             pltpu.VMEM((widest, inner), jnp.float32),
             dma((4,)),
             dma((chunks,)),
             dma((chunks,)),
             dma((2,)),
             dma((2,)),
-            dma((ticks, chunks)),
-            dma((ticks, parts, chunks)),
-            dma((ticks, chunks)),
-            dma((ticks, chunks)),
-            dma((ticks, chunks)),
-            dma((ticks, chunks)),
+            dma,
+            dma((ticks, sum(map(len, DISPATCH_RUNS)))),
+            dma,
+            dma((ticks, sum(map(len, RETURN_RUNS)))),
+            dma,
         ],
         compiler_params=pltpu.CompilerParams(
             collective_id=0, has_side_effects=True, vmem_limit_bytes=48 * 2**20

time: 48 us -> 46.6 us (0.971); the launches traced: 47.4 us -> 46.5 us
  Pallas kernels: 46.6 us -> 45.7 us
    pallas_call x1, Pallas kernels: 46.6 us -> 45.7 us  [on_device(): pl.pallas_call(functools.partial(relay_kernel, sections, experts), out_sh...]
where the time goes in v1:
time: 46.6 us; the launch traced here: 46.5 us
  Pallas kernels  45.7 us (98%)
  local copies, waits for them, and re-layouts  0.8 us (2%)
    pallas_call x1, Pallas kernels, on_device(): pl.pallas_call(functools.partial(relay_kernel, sections, experts), out_sh...  45.7 us

profile of v1, /device:TPU:0, one launch (start us, length us, event | category | flops | bytes accessed | tf_op | source)
XLA Modules:
  0.0 46.5 jit_solution(13034517096422311856)
XLA Ops:
  0.0 45.7 %relay.1 = bf16[1,128,2048]{2,1,0:T(8,128)(2,1)S(1)} custom-call(bf16[1,128,2048]{2,1,0:T(8,128)(2,1)} %state_hbm.1, f32[1,2048]{1,0:T(1,128)} %gain_hbm.1, bf16[1,1,2048,1536]{3,2,1,0:T(8,128)(2,1)} %win_hbm.1, bf16[1,1,768,2048]{3,2,1,0:T(8,128)(2,1)} %wout_hbm.1, s32[3,6,1,128]{3,2,1,0:T(1,128)} %bitcast.2, f32[3,6,1,128]{3,2,1,0:T(1,128)} %bitcast.3), custom_call_target="tpu_custom_call" | custom-call | tf_op jit(solution)/shard_map/relay/pallas_call | solution.py:394
  45.7 0.8 %copy.8 = bf16[1,128,2048]{2,1,0:T(8,128)(2,1)} copy(bf16[1,128,2048]{2,1,0:T(8,128)(2,1)S(1)} %relay.1) | data formatting | bytes 1048576

commit v2 on v1

--- a/solution.py
+++ b/solution.py
@@ -10,7 +10,7 @@
 epsilon = 1e-06
 COLUMN_SHARES = (1, 1, 1, 1)
 SLOT_SHARES = (1, 1)
-DISPATCH_RUNS = ((1, 1, 1, 1), (1, 1, 1, 1))
+DISPATCH_RUNS = ((1, 1, 1, 1), (2, 1, 1))
 RETURN_RUNS = ((2, 2), (1, 1, 1, 1))
 MESH = pl.DeviceIdType.MESH
 
@@ -55,8 +55,6 @@
     retsend,
     acc,
     load_sem,
-    win_sem,
-    state_sem,
     route_ss,
     route_rs,
     disp_ss,
@@ -124,19 +122,11 @@
     load_gain = pltpu.make_async_copy(gain_hbm, gain, load_sem.at[2])
     load_out = pltpu.make_async_copy(wout_hbm.at[0, 0], wout, load_sem.at[3])
 
-    def load_state(c):
-        cols = pl.ds(*columns[c])
-        return pltpu.make_async_copy(
-            state_hbm.at[0, :, cols], state.at[:, cols], state_sem.at[c]
-        )
-
-    def load_in(c):
-        rows = pl.ds(*columns[c])
-        return pltpu.make_async_copy(win_hbm.at[0, 0, rows], win.at[rows], win_sem.at[c])
+    load_state = pltpu.make_async_copy(state_hbm.at[0], state, load_sem.at[4])
+    load_in = pltpu.make_async_copy(win_hbm.at[0, 0], win, load_sem.at[5])
 
     load_ids.start()
-    for c in range(chunks):
-        load_state(c).start()
+    load_state.start()
     load_wts.start()
     load_gain.start()
 
@@ -287,19 +277,18 @@
 
     load_ids.wait()
     first[...] = kept_slots(ids, 0).astype(jnp.bfloat16)
+    load_state.wait()
+    load_in.start()
+    load_out.start()
     for c in range(chunks):
-        load_state(c).wait()
         fill(0, c, first[...], state[:, pl.ds(*columns[c])])
         keep_own(0, c)
-    for c in range(chunks):
-        load_in(c).start()
-    load_out.start()
     load_wts.wait()
     pl.semaphore_wait(barrier, experts - 1 + experts)
+    for c in range(chunks):
+        dispatch(0, c)
     for copy in route_copies():
         copy.start()
-    for c in range(chunks):
-        dispatch(0, c)
     for c in range(chunks):
         h_copy(0, c).start()
     for copy in route_copies():
@@ -317,8 +306,8 @@
             squares = jnp.zeros((group, 1), jnp.float32)
             for c in range(chunks):
                 cols = pl.ds(*columns[c])
-                if t == 0 and p == 0:
-                    load_in(c).wait()
+                if t == 0 and p == 0 and c == 0:
+                    load_in.wait()
                 await_rows(t, p, c)
                 wide = recvbuf[t, rows, cols].astype(jnp.float32)
                 squares = squares + jnp.sum(wide * wide, axis=-1, keepdims=True)
@@ -382,7 +371,6 @@
     hidden_units = expert_out.shape[2]
     slots = experts * (tokens // 4)
     columns = cuts(width, COLUMN_SHARES)
-    chunks = len(columns)
     widest = max(size for _, size in cuts(tokens // 4, SLOT_SHARES)) * experts
     bf16 = jnp.bfloat16
     hbm = pl.BlockSpec(memory_space=pltpu.HBM)
@@ -414,9 +402,7 @@
             pltpu.VMEM((ticks, slots, width), bf16),
             pltpu.VMEM((ticks, slots, width), bf16),
             pltpu.VMEM((widest, inner), jnp.float32),
-            dma((4,)),
-            dma((chunks,)),
-            dma((chunks,)),
+            dma((6,)),
             dma((2,)),
             dma((2,)),
             dma,

time: 46.6 us -> 46.6 us (level)
  no operation moved by 1% of the time
where the time goes in v2:
time: 46.6 us; the launch traced here: 46.4 us
  Pallas kernels  45.6 us (98%)
  local copies, waits for them, and re-layouts  0.8 us (2%)
    pallas_call x1, Pallas kernels, on_device(): pl.pallas_call(functools.partial(relay_kernel, sections, experts), out_sh...  45.6 us

profile of v2, /device:TPU:0, one launch (start us, length us, event | category | flops | bytes accessed | tf_op | source)
XLA Modules:
  0.0 46.4 jit_solution(5096241455921345247)
XLA Ops:
  0.0 45.6 %relay.1 = bf16[1,128,2048]{2,1,0:T(8,128)(2,1)S(1)} custom-call(bf16[1,128,2048]{2,1,0:T(8,128)(2,1)} %state_hbm.1, f32[1,2048]{1,0:T(1,128)} %gain_hbm.1, bf16[1,1,2048,1536]{3,2,1,0:T(8,128)(2,1)} %win_hbm.1, bf16[1,1,768,2048]{3,2,1,0:T(8,128)(2,1)} %wout_hbm.1, s32[3,6,1,128]{3,2,1,0:T(1,128)} %bitcast.2, f32[3,6,1,128]{3,2,1,0:T(1,128)} %bitcast.3), custom_call_target="tpu_custom_call" | custom-call | tf_op jit(solution)/shard_map/relay/pallas_call | solution.py:382
  45.6 0.8 %copy.8 = bf16[1,128,2048]{2,1,0:T(8,128)(2,1)} copy(bf16[1,128,2048]{2,1,0:T(8,128)(2,1)S(1)} %relay.1) | data formatting | bytes 1048576
